TPU v7x, 32 devices: a whole 2x2x4 slice. The times are simulated.
32 devices in a mesh: outer: 8 (over z, x), inner: 4 (over y, core).
Axes of the slice: x: 2, y: 2, z: 4, core: 2. Of those that a mesh axis runs over, the one named last changes fastest.
Arguments:
- queries: bfloat16 [1024, 2, 4096], P('outer', None, 'inner'), may hold values from -52 to 52
- keys: bfloat16 [1024, 2, 4096], P('outer', None, 'inner'), may hold values from -6 to 6
- values: bfloat16 [1024, 2, 4096], P('outer', None, 'inner'), may hold values from -6 to 6
Outputs:
- attended: bfloat16 [1024, 2, 4096], P(('outer', 'inner'))
All inputs are finite; a program needn't handle non-finite values.
Results may differ from a plain program's by a relative error of at most 0.004.
Values may be sent and summed in bfloat16 or wider, within the bound.
A program may use at most 128 MiB of HBM per device.

v0:
```python
from functools import partial
import math
import jax
import jax.numpy as jnp
from jax import lax
from jax.sharding import PartitionSpec as P

HEAD_DIM = 128


def attend_keys(running, key_block, value_block, query_heads, head_count):
    peak_rows, totals, numerator = running
    key_count = key_block.shape[0]
    key_heads = key_block.reshape(key_count, head_count, HEAD_DIM)
    value_heads = value_block.reshape(key_count, head_count, HEAD_DIM)
    scores = jnp.einsum(
        "qhd,khd->qhk", query_heads, key_heads, preferred_element_type=jnp.float32
    ) * (1.0 / math.sqrt(HEAD_DIM))
    new_peaks = jnp.maximum(peak_rows, jnp.max(scores, axis=2))
    shrink = jnp.exp(peak_rows - new_peaks)
    weights = jnp.exp(scores - new_peaks[..., None])
    totals = totals * shrink + jnp.sum(weights, axis=2)
    numerator = numerator * shrink[..., None] + jnp.einsum(
        "qhk,khd->qhd",
        weights.astype(jnp.bfloat16),
        value_heads,
        preferred_element_type=jnp.float32,
    )
    return (new_peaks, totals, numerator)


def attend_piece(running, pieces, start_row, query_part, head_count):
    key_rows, value_rows = pieces
    row_count = query_part.shape[0]
    query_heads = query_part.reshape(row_count, head_count, HEAD_DIM)
    block_count = key_rows.shape[0] // row_count
    key_blocks = key_rows.reshape(block_count, row_count, key_rows.shape[1])
    value_blocks = value_rows.reshape(block_count, row_count, value_rows.shape[1])

    def one_block(state, blocks):
        return (attend_keys(state, blocks[0], blocks[1], query_heads, head_count), None)

    running, unused = lax.scan(one_block, running, (key_blocks, value_blocks))
    return running


def start_state(row_count, head_count):
    peak_rows = jnp.full((row_count, head_count), -1e30, jnp.float32)
    totals = jnp.zeros((row_count, head_count), jnp.float32)
    numerator = jnp.zeros((row_count, head_count, HEAD_DIM), jnp.float32)
    return (peak_rows, totals, numerator)


def finish_state(running):
    peak_rows, totals, numerator = running
    averaged = numerator / totals[..., None]
    return averaged.reshape(numerator.shape[0], -1).astype(jnp.bfloat16)


def flatten(array):
    return array.reshape(array.shape[0], array.shape[1] * array.shape[2])


def per_device(queries, keys, values):
    tok_rows, networks, local_cols = queries.shape
    full_q, full_k, full_v = (
        lax.all_to_all(queries, "inner", split_axis=0, concat_axis=2, tiled=True),
        lax.all_to_all(keys, "inner", split_axis=0, concat_axis=2, tiled=True),
        lax.all_to_all(values, "inner", split_axis=0, concat_axis=2, tiled=True),
    )
    unit_rows = full_q.shape[0]
    full_cols = full_q.shape[2]
    query_part, key_part, value_part = (
        lax.all_to_all(flatten(full_q), "outer", split_axis=1, concat_axis=0, tiled=True),
        lax.all_to_all(flatten(full_k), "outer", split_axis=1, concat_axis=0, tiled=True),
        lax.all_to_all(flatten(full_v), "outer", split_axis=1, concat_axis=0, tiled=True),
    )
    head_count = query_part.shape[1] // HEAD_DIM
    folder = partial(attend_piece, query_part=query_part, head_count=head_count)
    running = folder(
        start_state(query_part.shape[0], head_count),
        (
            lax.all_gather(key_part, "inner", axis=0, tiled=True),
            lax.all_gather(value_part, "inner", axis=0, tiled=True),
        ),
        jnp.int32(0),
    )
    gathered = lax.all_to_all(
        finish_state(running), "outer", split_axis=0, concat_axis=1, tiled=True
    )
    attended = gathered.reshape(unit_rows, networks, full_cols)
    return attended


def solution(mesh):
    return jax.shard_map(
        per_device,
        mesh=mesh,
        in_specs=(P("outer", None, "inner"), P("outer", None, "inner"), P("outer", None, "inner")),
        out_specs=P(("outer", "inner"), None, None),
        check_vma=False,
    )
```

profile of v0, /device:TPU:0, one launch (start us, length us, event | category | flops | bytes accessed | tf_op | source)
XLA Modules:
  0.0 146.4 jit_solution(7811544565537679665)
XLA Ops:
  6.5 13.2 %all_to_all.112 = bf16[128,2,1024]{2,1,0:T(2,128)(2,1)S(1)} all-to-all(bf16[128,2,1024]{2,1,0:T(2,128)(2,1)} %param.6), channel_id=1, replica_groups=mesh['outer'=8,'inner'=4] {'inner'}, dimensions={0} | all-to-all | bytes 1048576 | tf_op jit(solution)/shard_map/all_to_all | solution.py:68
  19.9 20.5 %all_to_all.113 = bf16[32,8,1024]{2,0,1:T(8,128)(2,1)} all-to-all(bf16[32,8,1024]{2,0,1:T(8,128)(2,1)S(1)} %bitcast.72), channel_id=1, replica_groups=mesh['outer'=8,'inner'=4] {'outer'}, dimensions={1} | all-to-all | bytes 1048576 | tf_op jit(solution)/shard_map/all_to_all | solution.py:75
  40.4 14.9 %all_to_all.114 = bf16[128,2,1024]{2,1,0:T(2,128)(2,1)S(1)} all-to-all(bf16[128,2,1024]{2,1,0:T(2,128)(2,1)S(1)} %copy-done), channel_id=1, replica_groups=mesh['outer'=8,'inner'=4] {'inner'}, dimensions={0} | all-to-all | bytes 1048576 | tf_op jit(solution)/shard_map/all_to_all | solution.py:69
  55.5 17.2 %all_to_all.115 = bf16[32,8,1024]{2,0,1:T(8,128)(2,1)} all-to-all(bf16[32,8,1024]{2,0,1:T(8,128)(2,1)S(1)} %bitcast.73), channel_id=1, replica_groups=mesh['outer'=8,'inner'=4] {'outer'}, dimensions={1} | all-to-all | bytes 1048576 | tf_op jit(solution)/shard_map/all_to_all | solution.py:76
  72.7 14.9 %all_to_all.116 = bf16[128,2,1024]{2,1,0:T(2,128)(2,1)S(1)} all-to-all(bf16[128,2,1024]{2,1,0:T(2,128)(2,1)S(1)} %copy-done.1), channel_id=1, replica_groups=mesh['outer'=8,'inner'=4] {'inner'}, dimensions={0} | all-to-all | bytes 1048576 | tf_op jit(solution)/shard_map/all_to_all | solution.py:67
  87.5 0.9 copy.17
  88.5 3.5 %all-to-all-start.3 = ((bf16[32,8,1024]{2,0,1:T(8,128)(2,1)}), bf16[32,8,1024]{2,0,1:T(8,128)(2,1)S(1)}, u32[]{:S(2)}, u32[]{:S(2)}) async-start(bf16[32,8,1024]{2,0,1:T(8,128)(2,1)} %bitcast.8), calls=%async_computation.3 | async-start | bytes 1048576 | tf_op jit(solution)/shard_map/all_to_all | solution.py:74
  92.0 14.0 %all-to-all-done.3 = bf16[32,8,1024]{2,0,1:T(8,128)(2,1)S(1)} async-done(((bf16[32,8,1024]{2,0,1:T(8,128)(2,1)}), bf16[32,8,1024]{2,0,1:T(8,128)(2,1)S(1)}, u32[]{:S(2)}, u32[]{:S(2)}) %all-to-all-start.3) | async-done | bytes 524320 | tf_op jit(solution)/shard_map/all_to_all | solution.py:74
  106.3 13.4 %while.15 = (s32[]{:T(128)}, f32[256,8]{0,1:T(8,128)S(1)}, f32[256,8]{0,1:T(8,128)S(1)}, f32[256,8,128]{0,2,1:T(8,128)S(1)}, bf16[4,256,1024]{2,1,0:T(8,128)(2,1...) while((s32[]{:T(128)}, f32[256,8]{0,1:T(8,128)S(1)}, ...), condition=%wide.region_3.4_spmd.clone, body=%wide.region_0.3_spmd.clone.sunk | while | flops 273426432 | bytes 14286965 | solution.py:43
  106.3 1.3 constant_dynamic-slice_fusion.3
  107.5 0.2 copy.31
  108.0 0.5 bitcast_reduce_fusion.2
  108.5 0.4 fusion.23
  108.9 0.7 fusion.25
  109.6 1.3 constant_dynamic-slice_fusion.3
  110.9 0.2 copy.31
  111.3 0.5 bitcast_reduce_fusion.2
  111.8 0.4 fusion.23
  112.2 0.7 fusion.25
  113.0 1.3 constant_dynamic-slice_fusion.3
  114.7 0.5 bitcast_reduce_fusion.2
  115.2 0.4 fusion.23
  115.6 0.7 fusion.25
  116.3 1.3 constant_dynamic-slice_fusion.3
  118.0 0.5 bitcast_reduce_fusion.2
  118.5 0.4 fusion.23
  118.9 0.7 fusion.25
  119.7 0.3 copy.22
  120.1 0.2 convert_element_type.11
  120.3 17.9 %all_to_all.117 = bf16[8,32,1024]{2,1,0:T(8,128)(2,1)S(1)} all-to-all(bf16[8,32,1024]{2,1,0:T(8,128)(2,1)S(1)} %convert_element_type.11), channel_id=1, replica_groups=mesh['outer'=8,'inner'=4] {'outer'}, dimensions={0} | all-to-all | bytes 1048576 | tf_op jit(solution)/shard_map/all_to_all | solution.py:88
  138.2 0.3 copy.23
  138.5 1.1 reshape.52
  (36 shorter events, 1.9 us)
Async XLA Ops:
  6.5 33.9 %copy-start = (bf16[128,2,1024]{2,1,0:T(2,128)(2,1)S(1)}, bf16[128,2,1024]{2,1,0:T(2,128)(2,1)}, u32[]{:S(2)}) copy-start(bf16[128,2,1024]{2,1,0:T(2,128)(2,1)} %param.7) | copy-start | bytes 1572868
  6.5 99.7 %all-gather.3.cloned.1.call-start = ((), (), s32[]{:S(2)}) async-start(), calls=%async_computation.7 | async-start | bytes 2621440 | tf_op jit(solution)/shard_map/all_gather | solution.py:83
  40.3 32.3 %copy-start.1 = (bf16[128,2,1024]{2,1,0:T(2,128)(2,1)S(1)}, bf16[128,2,1024]{2,1,0:T(2,128)(2,1)}, u32[]{:S(2)}) copy-start(bf16[128,2,1024]{2,1,0:T(2,128)(2,1)} %param.5) | copy-start | bytes 1572868
  40.4 65.9 %all-gather.5.cloned.1.call-start = ((), (), s32[]{:S(2)}) async-start(), calls=%async_computation.8 | async-start | bytes 2621440 | tf_op jit(solution)/shard_map/all_gather | solution.py:84
  88.5 17.6 %all-to-all-start.3 = ((bf16[32,8,1024]{2,0,1:T(8,128)(2,1)}), bf16[32,8,1024]{2,0,1:T(8,128)(2,1)S(1)}, u32[]{:S(2)}, u32[]{:S(2)}) async-start(bf16[32,8,1024]{2,0,1:T(8,128)(2,1)} %bitcast.8), calls=%async_computation.3 | async-start | bytes 1048576 | tf_op jit(solution)/shard_map/all_to_all | solution.py:74
Sparse Core Ops, SparseCore 0:
  40.5 24.0 all-gather.2
  72.8 23.8 all-gather.4
where the time goes:
time: 147 us; the launch traced here: 146 us
  blocking collectives  98.5 us (67%)
  waiting for transfers between devices  14.1 us (10%)
  between operations  13.5 us (9%)
  local copies, waits for them, and re-layouts  10 us (7%)
  matrix products  4.86 us (3%)
  starting transfers between devices  3.54 us (2%)
  other arithmetic  1.62 us (1%)
    all_to_all x1, blocking collectives, per_device(): lax.all_to_all(flatten(full_k), 'outer', split_axis=1, concat_axis=0, til...  20.5 us
    all_to_all x1, blocking collectives, per_device(): lax.all_to_all(finish_state(running), 'outer', split_axis=0, concat_axis=...  17.9 us
    all_to_all x1, blocking collectives, per_device(): lax.all_to_all(flatten(full_v), 'outer', split_axis=1, concat_axis=0, til...  17.2 us
    all_to_all x1, blocking collectives, per_device(): lax.all_to_all(values, 'inner', split_axis=0, concat_axis=2, tiled=True)  14.9 us
    all_to_all x1, blocking collectives, per_device(): lax.all_to_all(queries, 'inner', split_axis=0, concat_axis=2, tiled=True)  14.9 us
    all_to_all x1, waiting for transfers between devices, per_device(): lax.all_to_all(flatten(full_q), 'outer', split_axis=1, concat_axis=0, til...  14 us
    all_to_all x1, blocking collectives, per_device(): lax.all_to_all(keys, 'inner', split_axis=0, concat_axis=2, tiled=True)  13.2 us
    dynamic_slice x12, local copies, waits for them, and re-layouts, attend_piece(): running, unused = lax.scan(one_block, running, (key_blocks, value_blocks))  6.72 us
  transfers between devices with their start and end apart: 3, of which 1 were waited for; matrix products, arithmetic and copies ran while one was open for 1% of the time, Pallas kernels for 0%

commit v1 on v0

--- a/solution.py
+++ b/solution.py
@@ -6,6 +6,28 @@
 from jax.sharding import PartitionSpec as P
 
 HEAD_DIM = 128
+
+
+def cut_along(value, dim, count):
+    before, after = (value.shape[:dim], value.shape[dim + 1 :])
+    return jnp.moveaxis(value.reshape(*before, count, -1, *after), dim, 0)
+
+
+def in_order(blocks, dim):
+    shape = list(blocks.shape[1:])
+    shape[dim] *= blocks.shape[0]
+    return jnp.moveaxis(blocks, 0, dim).reshape(shape)
+
+
+def exchange_directly(x, axis, split_dim, concat_dim):
+    size, index = (lax.axis_size(axis), lax.axis_index(axis))
+    blocks = cut_along(x, split_dim, size)
+    done = [blocks[index]]
+    for step in range(1, size):
+        sent = blocks[(index + step) % size]
+        done.append(lax.ppermute(sent, axis, [(i, (i + step) % size) for i in range(size)]))
+    blocks = jnp.stack(done)[(index - jnp.arange(size)) % size]
+    return in_order(blocks, concat_dim)
 
 
 def attend_keys(running, key_block, value_block, query_heads, head_count):
@@ -72,7 +94,7 @@
     full_cols = full_q.shape[2]
     query_part, key_part, value_part = (
         lax.all_to_all(flatten(full_q), "outer", split_axis=1, concat_axis=0, tiled=True),
-        lax.all_to_all(flatten(full_k), "outer", split_axis=1, concat_axis=0, tiled=True),
+        exchange_directly(flatten(full_k), "outer", 1, 0),
         lax.all_to_all(flatten(full_v), "outer", split_axis=1, concat_axis=0, tiled=True),
     )
     head_count = query_part.shape[1] // HEAD_DIM

time: 147 us -> 158 us (1.075)
  blocking collectives: 98.5 us -> 66.8 us
  waiting for transfers between devices: 14.1 us -> 40.7 us
  starting transfers between devices: 3.54 us -> 18 us
    all_to_all x2 -> x0, blocking collectives: 33.7 us -> none  [the longest x1 20.5 us: per_device(): lax.all_to_all(flatten(full_k), 'outer', split_axis=1, concat_axis=0, til...]
    ppermute x0 -> x7, waiting for transfers between devices: none -> 17.8 us  [exchange_directly(): lax.ppermute(sent, axis, [(i, (i + step) % size) for i in range(size)])]
    ppermute x0 -> x7, starting transfers between devices: none -> 10.2 us  [exchange_directly(): lax.ppermute(sent, axis, [(i, (i + step) % size) for i in range(size)])]
    all_to_all x0 -> x1, waiting for transfers between devices: none -> 8.77 us  [per_device(): lax.all_to_all(keys, 'inner', split_axis=0, concat_axis=2, tiled=True)]
    all_to_all x0 -> x1, starting transfers between devices: none -> 4.26 us  [per_device(): lax.all_to_all(keys, 'inner', split_axis=0, concat_axis=2, tiled=True)]
    all_to_all x1, blocking collectives: 14.9 us -> 16.9 us  [per_device(): lax.all_to_all(values, 'inner', split_axis=0, concat_axis=2, tiled=True)]
  transfers between devices with their start and end apart: 3 -> 11, of which waited for: 1 -> 5; matrix products, arithmetic and copies ran while one was open for 1% -> 1% of each run, Pallas kernels for 0% -> 0%
where the time goes in v1:
time: 158 us; the launch traced here: 157 us
  blocking collectives  66.8 us (42%)
  waiting for transfers between devices  40.7 us (26%)
  starting transfers between devices  18 us (11%)
  between operations  13.6 us (9%)
  local copies, waits for them, and re-layouts  11.5 us (7%)
  matrix products  4.89 us (3%)
  other arithmetic  1.64 us (1%)
    all_to_all x1, blocking collectives, per_device(): lax.all_to_all(finish_state(running), 'outer', split_axis=0, concat_axis=...  17.9 us
    ppermute x7, waiting for transfers between devices, exchange_directly(): lax.ppermute(sent, axis, [(i, (i + step) % size) for i in range(size)])  17.8 us
    all_to_all x1, blocking collectives, per_device(): lax.all_to_all(flatten(full_v), 'outer', split_axis=1, concat_axis=0, til...  17.2 us
    all_to_all x1, blocking collectives, per_device(): lax.all_to_all(values, 'inner', split_axis=0, concat_axis=2, tiled=True)  16.9 us
    all_to_all x1, blocking collectives, per_device(): lax.all_to_all(queries, 'inner', split_axis=0, concat_axis=2, tiled=True)  14.9 us
    all_to_all x1, waiting for transfers between devices, per_device(): lax.all_to_all(flatten(full_q), 'outer', split_axis=1, concat_axis=0, til...  14 us
    ppermute x7, starting transfers between devices, exchange_directly(): lax.ppermute(sent, axis, [(i, (i + step) % size) for i in range(size)])  10.2 us
    all_to_all x1, waiting for transfers between devices, per_device(): lax.all_to_all(keys, 'inner', split_axis=0, concat_axis=2, tiled=True)  8.77 us
  transfers between devices with their start and end apart: 11, of which 5 were waited for; matrix products, arithmetic and copies ran while one was open for 1% of the time, Pallas kernels for 0%

profile of v1, /device:TPU:0, one launch (start us, length us, event | category | flops | bytes accessed | tf_op | source)
XLA Modules:
  0.0 157.4 jit_solution(2468502306638037459)
XLA Ops:
  6.5 4.3 %all-to-all-start = ((bf16[128,2,1024]{2,1,0:T(2,128)(2,1)}), bf16[128,2,1024]{2,1,0:T(2,128)(2,1)S(1)}, u32[]{:S(2)}, u32[]{:S(2)}) async-start(bf16[128,2,1024]{2,1,0:T(2,128)(2,1)} %param.6), calls=%async_computation | async-start | bytes 1048576 | tf_op jit(solution)/shard_map/all_to_all | solution.py:90
  10.8 8.8 %all-to-all-done = bf16[128,2,1024]{2,1,0:T(2,128)(2,1)S(1)} async-done(((bf16[128,2,1024]{2,1,0:T(2,128)(2,1)}), bf16[128,2,1024]{2,1,0:T(2,128)(2,1)S(1)}, u32[]{:S(2)}, u32[]{:S(2)}) %all-to-all-start) | async-done | bytes 524320 | tf_op jit(solution)/shard_map/all_to_all | solution.py:90
  19.8 5.2 %collective-permute-start.6 = (bf16[32,1024]{1,0:T(8,128)(2,1)S(1)}, bf16[32,1024]{1,0:T(8,128)(2,1)S(1)}, u32[]{:S(2)}, u32[]{:S(2)}) collective-permute-start(bf16[32,1024]{1,0:T(8,128)(2,1)S(1)} %get-tuple-element.103), channel_id=1, source_target_pairs={{0,28},{4,0},{8,4},{12,8},{16,12},{20,16},{24,20},{28,24},{1,29},{... | collective-permute-start | bytes 196616 | tf_op jit(solution)/shard_map/ppermute | solution.py:28
  25.0 0.4 collective-permute-start.5
  25.5 3.0 %collective-permute-start.3 = (bf16[32,1024]{1,0:T(8,128)(2,1)S(1)}, bf16[32,1024]{1,0:T(8,128)(2,1)S(1)}, u32[]{:S(2)}, u32[]{:S(2)}) collective-permute-start(bf16[32,1024]{1,0:T(8,128)(2,1)S(1)} %get-tuple-element.106), channel_id=1, source_target_pairs={{0,16},{4,20},{8,24},{12,28},{16,0},{20,4},{24,8},{28,12},{1,17},{... | collective-permute-start | bytes 196616 | tf_op jit(solution)/shard_map/ppermute | solution.py:28
  28.5 1.5 collective-permute-start
  30.0 5.6 %collective-permute-done = bf16[32,1024]{1,0:T(8,128)(2,1)S(1)} collective-permute-done((bf16[32,1024]{1,0:T(8,128)(2,1)S(1)}, bf16[32,1024]{1,0:T(8,128)(2,1)S(1)}, u32[]{:S(2)}, u32[]{:S(2)}) %collective-permute-start) | collective-permute-done | bytes 65568 | tf_op jit(solution)/shard_map/ppermute | solution.py:28
  35.6 6.2 %collective-permute-done.1 = bf16[32,1024]{1,0:T(8,128)(2,1)S(1)} collective-permute-done((bf16[32,1024]{1,0:T(8,128)(2,1)S(1)}, bf16[32,1024]{1,0:T(8,128)(2,1)S(1)}, u32[]{:S(2)}, u32[]{:S(2)}) %collective-permute-start.1) | collective-permute-done | bytes 65568 | tf_op jit(solution)/shard_map/ppermute | solution.py:28
  41.8 6.1 %collective-permute-done.2 = bf16[32,1024]{1,0:T(8,128)(2,1)S(1)} collective-permute-done((bf16[32,1024]{1,0:T(8,128)(2,1)S(1)}, bf16[32,1024]{1,0:T(8,128)(2,1)S(1)}, u32[]{:S(2)}, u32[]{:S(2)}) %collective-permute-start.2) | collective-permute-done | bytes 65568 | tf_op jit(solution)/shard_map/ppermute | solution.py:28
  47.9 1.4 gather_fusion
  49.4 16.9 %all_to_all.93 = bf16[128,2,1024]{2,1,0:T(2,128)(2,1)S(1)} all-to-all(bf16[128,2,1024]{2,1,0:T(2,128)(2,1)S(1)} %copy-done), channel_id=1, replica_groups=mesh['outer'=8,'inner'=4] {'inner'}, dimensions={0} | all-to-all | bytes 1048576 | tf_op jit(solution)/shard_map/all_to_all | solution.py:91
  66.4 17.2 %all_to_all.94 = bf16[32,8,1024]{2,0,1:T(8,128)(2,1)} all-to-all(bf16[32,8,1024]{2,0,1:T(8,128)(2,1)S(1)} %bitcast.104), channel_id=1, replica_groups=mesh['outer'=8,'inner'=4] {'outer'}, dimensions={1} | all-to-all | bytes 1048576 | tf_op jit(solution)/shard_map/all_to_all | solution.py:98
  83.6 14.9 %all_to_all.95 = bf16[128,2,1024]{2,1,0:T(2,128)(2,1)S(1)} all-to-all(bf16[128,2,1024]{2,1,0:T(2,128)(2,1)S(1)} %copy-done.1), channel_id=1, replica_groups=mesh['outer'=8,'inner'=4] {'inner'}, dimensions={0} | all-to-all | bytes 1048576 | tf_op jit(solution)/shard_map/all_to_all | solution.py:89
  98.5 0.9 copy.17
  99.5 3.5 %all-to-all-start.2 = ((bf16[32,8,1024]{2,0,1:T(8,128)(2,1)}), bf16[32,8,1024]{2,0,1:T(8,128)(2,1)S(1)}, u32[]{:S(2)}, u32[]{:S(2)}) async-start(bf16[32,8,1024]{2,0,1:T(8,128)(2,1)} %bitcast.25), calls=%async_computation.2 | async-start | bytes 1048576 | tf_op jit(solution)/shard_map/all_to_all | solution.py:96
  103.0 14.0 %all-to-all-done.2 = bf16[32,8,1024]{2,0,1:T(8,128)(2,1)S(1)} async-done(((bf16[32,8,1024]{2,0,1:T(8,128)(2,1)}), bf16[32,8,1024]{2,0,1:T(8,128)(2,1)S(1)}, u32[]{:S(2)}, u32[]{:S(2)}) %all-to-all-start.2) | async-done | bytes 524320 | tf_op jit(solution)/shard_map/all_to_all | solution.py:96
  117.2 13.4 %while.15 = (s32[]{:T(128)}, f32[256,8]{0,1:T(8,128)S(1)}, f32[256,8]{0,1:T(8,128)S(1)}, f32[256,8,128]{0,2,1:T(8,128)S(1)}, bf16[4,256,1024]{2,1,0:T(8,128)(2,1...) while((s32[]{:T(128)}, f32[256,8]{0,1:T(8,128)S(1)}, ...), condition=%wide.region_3.4_spmd.clone, body=%wide.region_0.3_spmd.clone.sunk | while | flops 273426432 | bytes 14286965 | solution.py:65
  117.3 1.3 constant_dynamic-slice_fusion.3
  118.9 0.5 bitcast_reduce_fusion.2
  119.5 0.4 fusion.25
  119.8 0.7 fusion.27
  120.6 1.3 constant_dynamic-slice_fusion.3
  122.3 0.5 bitcast_reduce_fusion.2
  123.2 0.7 fusion.27
  124.0 1.3 constant_dynamic-slice_fusion.3
  125.7 0.5 bitcast_reduce_fusion.2
  126.6 0.7 fusion.27
  127.3 1.3 constant_dynamic-slice_fusion.3
  129.0 0.5 bitcast_reduce_fusion.2
  129.9 0.7 fusion.27
  131.3 17.9 %all_to_all.96 = bf16[8,32,1024]{2,1,0:T(8,128)(2,1)S(1)} all-to-all(bf16[8,32,1024]{2,1,0:T(8,128)(2,1)S(1)} %convert_element_type.11), channel_id=1, replica_groups=mesh['outer'=8,'inner'=4] {'outer'}, dimensions={0} | all-to-all | bytes 1048576 | tf_op jit(solution)/shard_map/all_to_all | solution.py:110
  149.5 1.1 reshape.115
  (62 shorter events, 4.4 us)
Async XLA Ops:
  6.5 13.1 %all-to-all-start = ((bf16[128,2,1024]{2,1,0:T(2,128)(2,1)}), bf16[128,2,1024]{2,1,0:T(2,128)(2,1)S(1)}, u32[]{:S(2)}, u32[]{:S(2)}) async-start(bf16[128,2,1024]{2,1,0:T(2,128)(2,1)} %param.6), calls=%async_computation | async-start | bytes 1048576 | tf_op jit(solution)/shard_map/all_to_all | solution.py:90
  10.8 106.4 %all-gather.3.cloned.1.call-start = ((), (), s32[]{:S(2)}) async-start(), calls=%async_computation.6 | async-start | bytes 2621440 | tf_op jit(solution)/shard_map/all_gather | solution.py:105
  10.8 38.6 %copy-start = (bf16[128,2,1024]{2,1,0:T(2,128)(2,1)S(1)}, bf16[128,2,1024]{2,1,0:T(2,128)(2,1)}, u32[]{:S(2)}) copy-start(bf16[128,2,1024]{2,1,0:T(2,128)(2,1)} %param.7) | copy-start | bytes 1572868
  19.8 28.1 %collective-permute-start.6 = (bf16[32,1024]{1,0:T(8,128)(2,1)S(1)}, bf16[32,1024]{1,0:T(8,128)(2,1)S(1)}, u32[]{:S(2)}, u32[]{:S(2)}) collective-permute-start(bf16[32,1024]{1,0:T(8,128)(2,1)S(1)} %get-tuple-element.103), channel_id=1, source_target_pairs={{0,28},{4,0},{8,4},{12,8},{16,12},{20,16},{24,20},{28,24},{1,29},{... | collective-permute-start | bytes 196616 | tf_op jit(solution)/shard_map/ppermute | solution.py:28
  25.0 22.9 %collective-permute-start.5 = (bf16[32,1024]{1,0:T(8,128)(2,1)S(1)}, bf16[32,1024]{1,0:T(8,128)(2,1)S(1)}, u32[]{:S(2)}, u32[]{:S(2)}) collective-permute-start(bf16[32,1024]{1,0:T(8,128)(2,1)S(1)} %get-tuple-element.104), channel_id=1, source_target_pairs={{0,24},{4,28},{8,0},{12,4},{16,8},{20,12},{24,16},{28,20},{1,25},{... | collective-permute-start | bytes 196616 | tf_op jit(solution)/shard_map/ppermute | solution.py:28
  25.5 22.4 %collective-permute-start.4 = (bf16[32,1024]{1,0:T(8,128)(2,1)S(1)}, bf16[32,1024]{1,0:T(8,128)(2,1)S(1)}, u32[]{:S(2)}, u32[]{:S(2)}) collective-permute-start(bf16[32,1024]{1,0:T(8,128)(2,1)S(1)} %get-tuple-element.105), channel_id=1, source_target_pairs={{0,20},{4,24},{8,28},{12,0},{16,4},{20,8},{24,12},{28,16},{1,21},{... | collective-permute-start | bytes 196616 | tf_op jit(solution)/shard_map/ppermute | solution.py:28
  25.5 22.4 %collective-permute-start.3 = (bf16[32,1024]{1,0:T(8,128)(2,1)S(1)}, bf16[32,1024]{1,0:T(8,128)(2,1)S(1)}, u32[]{:S(2)}, u32[]{:S(2)}) collective-permute-start(bf16[32,1024]{1,0:T(8,128)(2,1)S(1)} %get-tuple-element.106), channel_id=1, source_target_pairs={{0,16},{4,20},{8,24},{12,28},{16,0},{20,4},{24,8},{28,12},{1,17},{... | collective-permute-start | bytes 196616 | tf_op jit(solution)/shard_map/ppermute | solution.py:28
  28.5 7.1 %collective-permute-start = (bf16[32,1024]{1,0:T(8,128)(2,1)S(1)}, bf16[32,1024]{1,0:T(8,128)(2,1)S(1)}, u32[]{:S(2)}, u32[]{:S(2)}) collective-permute-start(bf16[32,1024]{1,0:T(8,128)(2,1)S(1)} %get-tuple-element.109), channel_id=1, source_target_pairs={{0,4},{4,8},{8,12},{12,16},{16,20},{20,24},{24,28},{28,0},{1,5},{5... | collective-permute-start | bytes 196616 | tf_op jit(solution)/shard_map/ppermute | solution.py:28
  35.6 6.2 %collective-permute-start.1 = (bf16[32,1024]{1,0:T(8,128)(2,1)S(1)}, bf16[32,1024]{1,0:T(8,128)(2,1)S(1)}, u32[]{:S(2)}, u32[]{:S(2)}) collective-permute-start(bf16[32,1024]{1,0:T(8,128)(2,1)S(1)} %get-tuple-element.108), channel_id=1, source_target_pairs={{0,8},{4,12},{8,16},{12,20},{16,24},{20,28},{24,0},{28,4},{1,9},{5... | collective-permute-start | bytes 196616 | tf_op jit(solution)/shard_map/ppermute | solution.py:28
  41.8 6.1 %collective-permute-start.2 = (bf16[32,1024]{1,0:T(8,128)(2,1)S(1)}, bf16[32,1024]{1,0:T(8,128)(2,1)S(1)}, u32[]{:S(2)}, u32[]{:S(2)}) collective-permute-start(bf16[32,1024]{1,0:T(8,128)(2,1)S(1)} %get-tuple-element.107), channel_id=1, source_target_pairs={{0,12},{4,16},{8,20},{12,24},{16,28},{20,0},{24,4},{28,8},{1,13},{... | collective-permute-start | bytes 196616 | tf_op jit(solution)/shard_map/ppermute | solution.py:28
  49.3 34.3 %copy-start.1 = (bf16[128,2,1024]{2,1,0:T(2,128)(2,1)S(1)}, bf16[128,2,1024]{2,1,0:T(2,128)(2,1)}, u32[]{:S(2)}) copy-start(bf16[128,2,1024]{2,1,0:T(2,128)(2,1)} %param.5) | copy-start | bytes 1572868
  49.3 67.9 %all-gather.5.cloned.1.call-start = ((), (), s32[]{:S(2)}) async-start(), calls=%async_computation.7 | async-start | bytes 2621440 | tf_op jit(solution)/shard_map/all_gather | solution.py:106
  99.5 17.6 %all-to-all-start.2 = ((bf16[32,8,1024]{2,0,1:T(8,128)(2,1)}), bf16[32,8,1024]{2,0,1:T(8,128)(2,1)S(1)}, u32[]{:S(2)}, u32[]{:S(2)}) async-start(bf16[32,8,1024]{2,0,1:T(8,128)(2,1)} %bitcast.25), calls=%async_computation.2 | async-start | bytes 1048576 | tf_op jit(solution)/shard_map/all_to_all | solution.py:96
Sparse Core Ops, SparseCore 0:
  49.5 24.0 all-gather.2
  83.8 23.8 all-gather.4
